TPU v7x, 32 devices: a whole 2x2x4 slice. The times are simulated.
32 devices in a mesh: section: 2 (over core), dev: 16 (over z, y, x).
Axes of the slice: x: 2, y: 2, z: 4, core: 2. Of those that a mesh axis runs over, the one named last changes fastest.
Arguments:
- indices: int32 [2048, 32, 8], P(('section', 'dev')), may hold values from 0 to 32767
- pool_len: int32 [32], replicated, may hold values from 1 to 8
- tables: bfloat16 [1048576, 128], P(('section', 'dev')), may hold values from -3 to 3
- w_first: bfloat16 [4096, 4096], P('dev', 'section'), may hold values from -0.09375 to 0.09375
- b_first: bfloat16 [4096], P('section'), may hold values from -3 to 3
- w_out: bfloat16 [4096], P('section'), may hold values from -0.09375 to 0.09375
Outputs:
- logits: float32 [2048], P('dev')
Inputs may be any that keep to these rules, and one draw needn't show every extreme that they name: `indices`: ids of rows of the table named by the second index.
All inputs are finite; a program needn't handle non-finite values.
Results may differ from a plain program's by a relative error of at most 0.0095.
Values may be sent and summed in bfloat16 or wider, within the bound.
A program may use at most 128 MiB of HBM per device.

v0:
```python
import jax
import jax.numpy as jnp
from jax import lax
from jax.sharding import PartitionSpec as P


def body(indices, pool_len, tables, w_first, b_first, w_out):
    sec_count = lax.axis_size("section")
    dev_count = lax.axis_size("dev")
    devices = sec_count * dev_count
    dev_rows, n_tables, pool_size = indices.shape
    rows_dev, emb_width = tables.shape
    row_split = devices // n_tables
    position = lax.axis_index("section") * dev_count + lax.axis_index("dev")
    table_id = position // row_split
    first_row = position % row_split * rows_dev
    outgoing = jnp.repeat(indices, row_split, axis=1)
    arrived = lax.all_to_all(outgoing, ("section", "dev"), split_axis=1, concat_axis=0, tiled=True)
    all_rows = devices * dev_rows
    wanted = arrived.reshape(all_rows, pool_size) - first_row
    live_slots = jnp.sum(jnp.where(jnp.arange(n_tables) == table_id, pool_len, 0))
    usable = (wanted >= 0) & (wanted < rows_dev) & (jnp.arange(pool_size)[None, :] < live_slots)
    safe_rows = jnp.where(usable, wanted, 0)
    looked = jnp.take(tables, safe_rows, axis=0)
    picked = jnp.where(usable[:, :, None], looked, jnp.zeros((), jnp.bfloat16))
    partial_value = jnp.sum(picked.astype(jnp.float32), axis=1).astype(jnp.bfloat16)
    ordered = jnp.transpose(
        partial_value.reshape(dev_count, sec_count, dev_rows, emb_width), (1, 0, 2, 3)
    )
    received = lax.all_to_all(
        ordered.reshape(devices, dev_rows, emb_width),
        ("section", "dev"),
        split_axis=0,
        concat_axis=0,
        tiled=True,
    )
    summed = jnp.sum(
        received.reshape(n_tables, row_split, dev_rows, emb_width).astype(jnp.float32), axis=1
    )
    features = jnp.transpose(summed.astype(jnp.bfloat16), (1, 0, 2)).reshape(
        dev_rows, n_tables * emb_width
    )
    samples = lax.all_gather(features, "section", axis=0, tiled=True)
    whole_weights = lax.all_gather(w_first, "dev", axis=0, tiled=True)
    pre_act = jnp.dot(samples, whole_weights, preferred_element_type=jnp.float32)
    hidden = jnp.maximum(pre_act + b_first.astype(jnp.float32)[None, :], 0.0)
    logit_part = jnp.sum(hidden * w_out.astype(jnp.float32)[None, :], axis=1)
    return lax.psum(logit_part, "section")


def solution(mesh):
    placed = (
        P(("section", "dev"), None, None),
        P(),
        P(("section", "dev"), None),
        P("dev", "section"),
        P("section"),
        P("section"),
    )
    return jax.shard_map(body, mesh=mesh, in_specs=placed, out_specs=P("dev"), check_vma=False)
```

profile of v0, /device:TPU:0, one launch (start us, length us, event | category | flops | bytes accessed | tf_op | source)
XLA Modules:
  0.0 337.2 jit_solution(18316282832456618671)
XLA Ops:
  6.5 1.6 reshape.131
  8.2 7.3 %all-to-all-start = ((s32[32,1,512]{2,1,0:T(1,128)}), s32[32,1,512]{2,1,0:T(1,128)S(1)}, u32[]{:S(2)}, u32[]{:S(2)}) async-start(s32[32,1,512]{2,1,0:T(1,128)} %reshape.131), calls=%async_computation | async-start | bytes 131072 | tf_op jit(solution)/shard_map/all_to_all | solution.py:18
  15.5 0.0 all-gather.3.cloned.1.call-start
  15.6 1.3 fusion.5
  16.9 0.6 iota_compare_fusion
  17.5 5.3 %all-to-all-done = s32[32,1,512]{2,1,0:T(1,128)S(1)} async-done(((s32[32,1,512]{2,1,0:T(1,128)}), s32[32,1,512]{2,1,0:T(1,128)S(1)}, u32[]{:S(2)}, u32[]{:S(2)}) %all-to-all-start) | async-done | bytes 65568 | tf_op jit(solution)/shard_map/all_to_all | solution.py:18
  22.8 0.5 broadcast.97
  23.4 0.8 reduce.1
  24.2 0.1 reshape.132
  24.3 0.1 reshape.117
  24.4 0.1 reshape.118
  24.5 0.1 and_and_fusion
  24.6 0.4 copy.14
  25.0 0.4 copy.15
  25.5 0.1 compare_select_fusion
  25.6 0.3 copy.17
  25.9 0.5 reshape.124
  26.4 59.4 %gather_fusion = bf16[16384,128]{1,0:T(8,128)(2,1)} fusion(bf16[32768,128]{1,0:T(8,128)(2,1)} %param.8, s32[16384]{0:T(1024)S(1)} %broadcast_clamp_fusion), kind=kCustom, calls=%fused_computation | custom fusion | bytes 8454144 | tf_op jit(solution)/shard_map/jit(_take)/gather | solution.py:24
  85.8 0.0 copy-start
  85.8 0.0 copy-start.1
  85.8 12.6 %fusion.1 = bf16[2048,128]{1,0:T(8,128)(2,1)S(1)} fusion(bf16[16384,128]{1,0:T(8,128)(2,1)} %gather_fusion, pred[2048,8]{1,0:T(8,128)(4,1)S(1)} %copy.15, pred[2048,8]{1,0:T(8,128)(4,1)S(1)} %copy.14), kind=kLoop, calls=%fused_computation.3 | loop fusion | flops 6029312 | bytes 4751360 | tf_op jit(solution)/shard_map/reduce_sum | solution.py:26
  98.5 18.5 %all_to_all.20 = bf16[32,64,128]{2,1,0:T(8,128)(2,1)S(1)} all-to-all(bf16[32,64,128]{2,1,0:T(8,128)(2,1)S(1)} %bitcast.36), channel_id=1, replica_groups=mesh['section'=2,'dev'=16] {'section','dev'}, dimensions={0} | all-to-all | bytes 1048576 | tf_op jit(solution)/shard_map/all_to_all | solution.py:30
  117.1 0.9 copy_bitcast_fusion
  118.0 0.0 all-gather.3.cloned.1.call-update
  118.0 0.0 all-gather.5.cloned.1.call-start
  118.0 0.7 all-gather.5.cloned.1.call-update
  118.7 0.0 copy-done
  118.8 0.0 copy-done.1
  118.8 5.0 %all-gather.3.cloned.1.call-done = bf16[128,4096]{1,0:T(8,128)(2,1)} async-done(((bf16[64,4096]{1,0:T(8,128)(2,1)}), bf16[128,4096]{1,0:T(8,128)(2,1)}) %all-gather.3.cloned.1.call-update) | async-done | bytes 1048592 | tf_op jit(solution)/shard_map/all_gather | solution.py:43
  123.8 195.0 %all-gather.5.cloned.1.call-done = bf16[4096,2048]{1,0:T(8,128)(2,1)} async-done(((bf16[256,2048]{1,0:T(8,128)(2,1)}), bf16[4096,2048]{1,0:T(8,128)(2,1)}) %all-gather.5.cloned.1.call-update) | async-done | bytes 16777232 | tf_op jit(solution)/shard_map/all_gather | solution.py:44
  318.8 8.6 %fusion.4 = f32[128]{0:T(128)S(1)} fusion(bf16[128,4096]{1,0:T(8,128)(2,1)} %all-gather.3.cloned.1.call-done, bf16[4096,2048]{1,0:T(8,128)(2,1)} %all-gather.5.cloned.1.call-done, f32[2048]{0:T(1024)S(1)} %convert_element_type.12, f32[2048]{0:T(1024)S(1)} %convert_element_type.5), kind=kOutput, calls=%fused_computation.7 | convolution fusion | flops 2148532224 | bytes 17842688 | tf_op jit(solution)/shard_map/dot_general | solution.py:45
  327.4 3.0 psum.7
  (6 shorter events, 0.1 us)
Async XLA Ops:
  8.2 14.7 %all-to-all-start = ((s32[32,1,512]{2,1,0:T(1,128)}), s32[32,1,512]{2,1,0:T(1,128)S(1)}, u32[]{:S(2)}, u32[]{:S(2)}) async-start(s32[32,1,512]{2,1,0:T(1,128)} %reshape.131), calls=%async_computation | async-start | bytes 131072 | tf_op jit(solution)/shard_map/all_to_all | solution.py:18
  15.5 108.3 %all-gather.3.cloned.1.call-start = ((), (), s32[]{:S(2)}) async-start(), calls=%async_computation.2 | async-start | bytes 1572864 | tf_op jit(solution)/shard_map/all_gather | solution.py:43
  85.8 32.9 %copy-start = (bf16[2048]{0:T(1024)(128)(2,1)S(1)}, bf16[2048]{0:T(1024)(128)(2,1)}, u32[]{:S(2)}) copy-start(bf16[2048]{0:T(1024)(128)(2,1)} %param.11) | copy-start | bytes 12292
  85.8 32.9 %copy-start.1 = (bf16[2048]{0:T(1024)(128)(2,1)S(1)}, bf16[2048]{0:T(1024)(128)(2,1)}, u32[]{:S(2)}) copy-start(bf16[2048]{0:T(1024)(128)(2,1)} %param.10) | copy-start | bytes 12292
  118.0 200.8 %all-gather.5.cloned.1.call-start = ((), (), s32[]{:S(2)}) async-start(), calls=%async_computation.3 | async-start | bytes 17825792 | tf_op jit(solution)/shard_map/all_gather | solution.py:44
Sparse Core Ops, SparseCore 0:
  118.1 5.6 all-gather.2
  126.6 192.1 all-gather.4
where the time goes:
time: 337 us
  waiting for transfers between devices  206 us (61%)
  local copies, waits for them, and re-layouts  64.5 us (19%)
  blocking collectives  21.5 us (6%)
  other arithmetic  15.6 us (5%)
  between operations  13.5 us (4%)
  matrix products  8.58 us (3%)
  starting transfers between devices  7.41 us (2%)
    all_gather x1, waiting for transfers between devices, body(): whole_weights = lax.all_gather(w_first, 'dev', axis=0, tiled=True)  195 us
    gather x1, local copies, waits for them, and re-layouts, body(): looked = jnp.take(tables, safe_rows, axis=0)  59.4 us
    all_to_all x1, blocking collectives, body(): lax.all_to_all(ordered.reshape(devices, dev_rows, emb_width), ('section',...  18.5 us
    reduce_sum x1, other arithmetic, body(): jnp.sum(picked.astype(jnp.float32), axis=1).astype(jnp.bfloat16)  12.6 us
    dot_general x1, matrix products, body(): jnp.dot(samples, whole_weights, preferred_element_type=jnp.float32)  8.58 us
    all_to_all x1, starting transfers between devices, body(): lax.all_to_all(outgoing, ('section', 'dev'), split_axis=1, concat_axis=0,...  7.33 us
  transfers between devices with their start and end apart: 3, of which 3 were waited for; matrix products, arithmetic and copies ran while one was open for 1% of the time, Pallas kernels for 0%

commit v1 on v0

--- a/solution.py
+++ b/solution.py
@@ -41,7 +41,12 @@
         dev_rows, n_tables * emb_width
     )
     samples = lax.all_gather(features, "section", axis=0, tiled=True)
-    whole_weights = lax.all_gather(w_first, "dev", axis=0, tiled=True)
+    ring = [w_first]
+    for hop in range(15):
+        ring.append(lax.ppermute(ring[-1], "dev", [(dev, (dev + 1) % 16) for dev in range(16)]))
+    whole_weights = jnp.roll(
+        jnp.concatenate(ring[::-1], axis=0), (lax.axis_index("dev") + 1) * ring[0].shape[0], axis=0
+    )
     pre_act = jnp.dot(samples, whole_weights, preferred_element_type=jnp.float32)
     hidden = jnp.maximum(pre_act + b_first.astype(jnp.float32)[None, :], 0.0)
     logit_part = jnp.sum(hidden * w_out.astype(jnp.float32)[None, :], axis=1)

time: 337 us -> 521 us (1.55)
  waiting for transfers between devices: 206 us -> 326 us
  local copies, waits for them, and re-layouts: 64.5 us -> 135 us
  blocking collectives: 21.5 us -> 2.97 us
  starting transfers between devices: 7.41 us -> 15.6 us
    ppermute x0 -> x15, waiting for transfers between devices: none -> 283 us  [body(): lax.ppermute(ring[-1], 'dev', [(dev, (dev + 1) % 16) for dev in range(16)])]
    all_gather x1 -> x0, waiting for transfers between devices: 195 us -> none  [body(): whole_weights = lax.all_gather(w_first, 'dev', axis=0, tiled=True)]
    unnamed x6 -> x77, local copies, waits for them, and re-layouts: 1.74 us -> 65.7 us
    all_to_all x0 -> x1, waiting for transfers between devices: none -> 31.9 us  [body(): lax.all_to_all(ordered.reshape(devices, dev_rows, emb_width), ('section',...]
    all_to_all x1 -> x0, blocking collectives: 18.5 us -> none  [body(): lax.all_to_all(ordered.reshape(devices, dev_rows, emb_width), ('section',...]
    all_to_all x1, waiting for transfers between devices: 5.32 us -> 11.2 us  [body(): lax.all_to_all(outgoing, ('section', 'dev'), split_axis=1, concat_axis=0,...]
  transfers between devices with their start and end apart: 3 -> 18, of which waited for: 3 -> 14; matrix products, arithmetic and copies ran while one was open for 1% -> 28% of each run, Pallas kernels for 0% -> 0%
where the time goes in v1:
time: 521 us; the launch traced here: 519 us
  waiting for transfers between devices  326 us (63%)
  local copies, waits for them, and re-layouts  135 us (26%)
  other arithmetic  17 us (3%)
  starting transfers between devices  15.6 us (3%)
  between operations  13.7 us (3%)
  matrix products  8.58 us (2%)
    ppermute x15, waiting for transfers between devices, body(): lax.ppermute(ring[-1], 'dev', [(dev, (dev + 1) % 16) for dev in range(16)])  283 us
    unnamed x77, local copies, waits for them, and re-layouts  65.7 us
    gather x1, local copies, waits for them, and re-layouts, body(): looked = jnp.take(tables, safe_rows, axis=0)  59.9 us
    all_to_all x1, waiting for transfers between devices, body(): lax.all_to_all(ordered.reshape(devices, dev_rows, emb_width), ('section',...  31.9 us
    reduce_sum x1, other arithmetic, body(): jnp.sum(picked.astype(jnp.float32), axis=1).astype(jnp.bfloat16)  12.8 us
    all_to_all x1, waiting for transfers between devices, body(): lax.all_to_all(outgoing, ('section', 'dev'), split_axis=1, concat_axis=0,...  11.2 us
  transfers between devices with their start and end apart: 18, of which 14 were waited for; matrix products, arithmetic and copies ran while one was open for 28% of the time, Pallas kernels for 0%

profile of v1, /device:TPU:0, one launch (start us, length us, event | category | flops | bytes accessed | tf_op | source)
XLA Modules:
  0.0 519.5 jit_solution(1589710731771580113)
XLA Ops:
  6.5 3.0 collective-permute-start
  9.5 27.4 %collective-permute-done = bf16[256,2048]{1,0:T(8,128)(2,1)S(1)} collective-permute-done((bf16[256,2048]{1,0:T(8,128)(2,1)}, bf16[256,2048]{1,0:T(8,128)(2,1)S(1)}, u32[]{:S(2)}, u32[]{:S(2)}) %collective-permute-start) | collective-permute-done | bytes 1048608 | tf_op jit(solution)/shard_map/ppermute | solution.py:46
  36.9 27.9 %collective-permute-done.1 = bf16[256,2048]{1,0:T(8,128)(2,1)S(1)} collective-permute-done((bf16[256,2048]{1,0:T(8,128)(2,1)S(1)}, bf16[256,2048]{1,0:T(8,128)(2,1)S(1)}, u32[]{:S(2)}, u32[]{:S(2)}) %collective-permute-start.1) | collective-permute-done | bytes 1048608 | tf_op jit(solution)/shard_map/ppermute | solution.py:46
  64.8 27.1 %collective-permute-done.2 = bf16[256,2048]{1,0:T(8,128)(2,1)S(1)} collective-permute-done((bf16[256,2048]{1,0:T(8,128)(2,1)S(1)}, bf16[256,2048]{1,0:T(8,128)(2,1)S(1)}, u32[]{:S(2)}, u32[]{:S(2)}) %collective-permute-start.2) | collective-permute-done | bytes 1048608 | tf_op jit(solution)/shard_map/ppermute | solution.py:46
  92.8 26.2 %collective-permute-done.3 = bf16[256,2048]{1,0:T(8,128)(2,1)S(1)} collective-permute-done((bf16[256,2048]{1,0:T(8,128)(2,1)S(1)}, bf16[256,2048]{1,0:T(8,128)(2,1)S(1)}, u32[]{:S(2)}, u32[]{:S(2)}) %collective-permute-start.3) | collective-permute-done | bytes 1048608 | tf_op jit(solution)/shard_map/ppermute | solution.py:46
  120.0 25.3 %collective-permute-done.4 = bf16[256,2048]{1,0:T(8,128)(2,1)S(1)} collective-permute-done((bf16[256,2048]{1,0:T(8,128)(2,1)S(1)}, bf16[256,2048]{1,0:T(8,128)(2,1)S(1)}, u32[]{:S(2)}, u32[]{:S(2)}) %collective-permute-start.4) | collective-permute-done | bytes 1048608 | tf_op jit(solution)/shard_map/ppermute | solution.py:46
  146.4 24.5 %collective-permute-done.5 = bf16[256,2048]{1,0:T(8,128)(2,1)S(1)} collective-permute-done((bf16[256,2048]{1,0:T(8,128)(2,1)S(1)}, bf16[256,2048]{1,0:T(8,128)(2,1)S(1)}, u32[]{:S(2)}, u32[]{:S(2)}) %collective-permute-start.5) | collective-permute-done | bytes 1048608 | tf_op jit(solution)/shard_map/ppermute | solution.py:46
  171.8 23.6 %collective-permute-done.6 = bf16[256,2048]{1,0:T(8,128)(2,1)S(1)} collective-permute-done((bf16[256,2048]{1,0:T(8,128)(2,1)S(1)}, bf16[256,2048]{1,0:T(8,128)(2,1)S(1)}, u32[]{:S(2)}, u32[]{:S(2)}) %collective-permute-start.6) | collective-permute-done | bytes 1048608 | tf_op jit(solution)/shard_map/ppermute | solution.py:46
  196.5 22.8 %collective-permute-done.7 = bf16[256,2048]{1,0:T(8,128)(2,1)S(1)} collective-permute-done((bf16[256,2048]{1,0:T(8,128)(2,1)S(1)}, bf16[256,2048]{1,0:T(8,128)(2,1)S(1)}, u32[]{:S(2)}, u32[]{:S(2)}) %collective-permute-start.7) | collective-permute-done | bytes 1048608 | tf_op jit(solution)/shard_map/ppermute | solution.py:46
  220.2 22.3 %collective-permute-done.8 = bf16[256,2048]{1,0:T(8,128)(2,1)S(1)} collective-permute-done((bf16[256,2048]{1,0:T(8,128)(2,1)S(1)}, bf16[256,2048]{1,0:T(8,128)(2,1)S(1)}, u32[]{:S(2)}, u32[]{:S(2)}) %collective-permute-start.8) | collective-permute-done | bytes 1048608 | tf_op jit(solution)/shard_map/ppermute | solution.py:46
  243.5 22.4 %collective-permute-done.9 = bf16[256,2048]{1,0:T(8,128)(2,1)S(1)} collective-permute-done((bf16[256,2048]{1,0:T(8,128)(2,1)S(1)}, bf16[256,2048]{1,0:T(8,128)(2,1)S(1)}, u32[]{:S(2)}, u32[]{:S(2)}) %collective-permute-start.9) | collective-permute-done | bytes 1048608 | tf_op jit(solution)/shard_map/ppermute | solution.py:46
  266.9 23.3 %collective-permute-done.10 = bf16[256,2048]{1,0:T(8,128)(2,1)S(1)} collective-permute-done((bf16[256,2048]{1,0:T(8,128)(2,1)S(1)}, bf16[256,2048]{1,0:T(8,128)(2,1)S(1)}, u32[]{:S(2)}, u32[]{:S(2)}) %collective-permute-start.10) | collective-permute-done | bytes 1048608 | tf_op jit(solution)/shard_map/ppermute | solution.py:46
  290.2 1.8 reshape.131
  292.0 5.9 %all-to-all-start = ((s32[32,1,512]{2,1,0:T(1,128)}), s32[32,1,512]{2,1,0:T(1,128)S(1)}, u32[]{:S(2)}, u32[]{:S(2)}) async-start(s32[32,1,512]{2,1,0:T(1,128)} %reshape.131), calls=%async_computation | async-start | bytes 131072 | tf_op jit(solution)/shard_map/all_to_all | solution.py:18
  297.8 1.3 fusion.16
  299.8 11.2 %all-to-all-done = s32[32,1,512]{2,1,0:T(1,128)S(1)} async-done(((s32[32,1,512]{2,1,0:T(1,128)}), s32[32,1,512]{2,1,0:T(1,128)S(1)}, u32[]{:S(2)}, u32[]{:S(2)}) %all-to-all-start) | async-done | bytes 65568 | tf_op jit(solution)/shard_map/all_to_all | solution.py:18
  313.5 1.2 copy.14
  316.5 1.3 copy.17
  317.8 1.6 reshape.124
  319.5 59.9 %gather_fusion = bf16[16384,128]{1,0:T(8,128)(2,1)} fusion(bf16[32768,128]{1,0:T(8,128)(2,1)} %param.8, s32[16384]{0:T(1024)S(1)} %broadcast_clamp_fusion), kind=kCustom, calls=%fused_computation | custom fusion | bytes 8454144 | tf_op jit(solution)/shard_map/jit(_take)/gather | solution.py:24
  379.4 1.8 collective-permute-start.13
  381.2 12.8 %fusion.3 = bf16[2048,128]{1,0:T(8,128)(2,1)S(1)} fusion(bf16[16384,128]{1,0:T(8,128)(2,1)} %gather_fusion, pred[2048,8]{1,0:T(8,128)(4,1)} %copy.15, pred[2048,8]{1,0:T(8,128)(4,1)S(1)} %copy.14), kind=kLoop, calls=%fused_computation.5 | loop fusion | flops 6029312 | bytes 4751360 | tf_op jit(solution)/shard_map/reduce_sum | solution.py:26
  394.9 4.7 all-to-all-start.1
  399.7 10.3 %collective-permute-done.13 = bf16[256,2048]{1,0:T(8,128)(2,1)} collective-permute-done((bf16[256,2048]{1,0:T(8,128)(2,1)}, bf16[256,2048]{1,0:T(8,128)(2,1)}, u32[]{:S(2)}, u32[]{:S(2)}) %collective-permute-start.13) | collective-permute-done | bytes 1048608 | tf_op jit(solution)/shard_map/ppermute | solution.py:46
  410.1 31.9 %all-to-all-done.1 = bf16[32,64,128]{2,1,0:T(8,128)(2,1)} async-done(((bf16[32,64,128]{2,1,0:T(8,128)(2,1)}), bf16[32,64,128]{2,1,0:T(8,128)(2,1)}, u32[]{:S(2)}, u32[]{:S(2)}) %all-to-all-start.1) | async-done | bytes 524320 | tf_op jit(solution)/shard_map/all_to_all | solution.py:30
  442.0 1.9 copy_bitcast_fusion
  444.0 2.5 constant_dynamic-update-slice_fusion.31
  446.5 3.3 constant_dynamic-update-slice_fusion.30
  449.8 2.3 constant_dynamic-update-slice_fusion.29
  452.1 2.3 constant_dynamic-update-slice_fusion.28
  454.4 2.3 constant_dynamic-update-slice_fusion.27
  456.8 2.3 constant_dynamic-update-slice_fusion.26
  459.1 2.3 constant_dynamic-update-slice_fusion.25
  461.4 2.4 constant_dynamic-update-slice_fusion.24
  463.8 2.4 constant_dynamic-update-slice_fusion.23
  466.2 2.3 constant_dynamic-update-slice_fusion.22
  468.5 2.3 constant_dynamic-update-slice_fusion.21
  470.8 2.3 constant_dynamic-update-slice_fusion.20
  473.2 2.3 constant_dynamic-update-slice_fusion.19
  476.6 1.1 constant_dynamic-update-slice_fusion.17
  478.8 2.3 constant_dynamic-update-slice_fusion.15
  481.1 2.3 constant_dynamic-update-slice_fusion.14
  483.4 2.3 constant_dynamic-update-slice_fusion.13
  485.7 2.3 constant_dynamic-update-slice_fusion.12
  491.2 1.1 constant_dynamic-update-slice_fusion.8
  498.8 1.1 constant_dynamic-update-slice_fusion.1
  501.1 8.6 %fusion.13 = f32[128]{0:T(128)S(1)} fusion(bf16[128,4096]{1,0:T(8,128)(2,1)} %all-gather.2.cloned.1.call-done, bf16[8192,2048]{1,0:T(8,128)(2,1)} %constant_dynamic-update-slice_fusion, s32[]{:T(128)S(6)} %select_n.70, f32[2048]{0:T(1024)S(1)} %convert_element_type.12, f32[2048]{0:T(1024)S(1)} %convert_element_type.5), kind=kOutput, calls=%fused_computation.9 | convolution fusion | flops 2148532224 | bytes 17842692 | tf_op jit(solution)/shard_map/dot_general | solution.py:50
  509.6 3.0 psum.7
  (90 shorter events, 26.8 us)
Async XLA Ops:
  6.5 30.3 %collective-permute-start = (bf16[256,2048]{1,0:T(8,128)(2,1)}, bf16[256,2048]{1,0:T(8,128)(2,1)S(1)}, u32[]{:S(2)}, u32[]{:S(2)}) collective-permute-start(bf16[256,2048]{1,0:T(8,128)(2,1)} %param.9), channel_id=1, source_target_pairs={{0,1},{1,2},{2,3},{3,4},{4,5},{5,6},{6,7},{7,8},{8,9},{9,10},{10,1... | collective-permute-start | bytes 3145736 | tf_op jit(solution)/shard_map/ppermute | solution.py:46
  36.9 27.9 %collective-permute-start.1 = (bf16[256,2048]{1,0:T(8,128)(2,1)S(1)}, bf16[256,2048]{1,0:T(8,128)(2,1)S(1)}, u32[]{:S(2)}, u32[]{:S(2)}) collective-permute-start(bf16[256,2048]{1,0:T(8,128)(2,1)S(1)} %collective-permute-done), channel_id=1, source_target_pairs={{0,1},{1,2},{2,3},{3,4},{4,5},{5,6},{6,7},{7,8},{8,9},{9,10},{10,1... | collective-permute-start | bytes 3145736 | tf_op jit(solution)/shard_map/ppermute | solution.py:46
  64.8 27.1 %collective-permute-start.2 = (bf16[256,2048]{1,0:T(8,128)(2,1)S(1)}, bf16[256,2048]{1,0:T(8,128)(2,1)S(1)}, u32[]{:S(2)}, u32[]{:S(2)}) collective-permute-start(bf16[256,2048]{1,0:T(8,128)(2,1)S(1)} %collective-permute-done.1), channel_id=1, source_target_pairs={{0,1},{1,2},{2,3},{3,4},{4,5},{5,6},{6,7},{7,8},{8,9},{9,10},{10,1... | collective-permute-start | bytes 3145736 | tf_op jit(solution)/shard_map/ppermute | solution.py:46
  91.8 1.0 copy-start.1
  92.8 26.2 %collective-permute-start.3 = (bf16[256,2048]{1,0:T(8,128)(2,1)S(1)}, bf16[256,2048]{1,0:T(8,128)(2,1)S(1)}, u32[]{:S(2)}, u32[]{:S(2)}) collective-permute-start(bf16[256,2048]{1,0:T(8,128)(2,1)S(1)} %collective-permute-done.2), channel_id=1, source_target_pairs={{0,1},{1,2},{2,3},{3,4},{4,5},{5,6},{6,7},{7,8},{8,9},{9,10},{10,1... | collective-permute-start | bytes 3145736 | tf_op jit(solution)/shard_map/ppermute | solution.py:46
  119.0 1.0 copy-start.3
  120.0 25.4 %collective-permute-start.4 = (bf16[256,2048]{1,0:T(8,128)(2,1)S(1)}, bf16[256,2048]{1,0:T(8,128)(2,1)S(1)}, u32[]{:S(2)}, u32[]{:S(2)}) collective-permute-start(bf16[256,2048]{1,0:T(8,128)(2,1)S(1)} %collective-permute-done.3), channel_id=1, source_target_pairs={{0,1},{1,2},{2,3},{3,4},{4,5},{5,6},{6,7},{7,8},{8,9},{9,10},{10,1... | collective-permute-start | bytes 3145736 | tf_op jit(solution)/shard_map/ppermute | solution.py:46
  145.4 1.0 copy-start.5
  146.4 24.5 %collective-permute-start.5 = (bf16[256,2048]{1,0:T(8,128)(2,1)S(1)}, bf16[256,2048]{1,0:T(8,128)(2,1)S(1)}, u32[]{:S(2)}, u32[]{:S(2)}) collective-permute-start(bf16[256,2048]{1,0:T(8,128)(2,1)S(1)} %collective-permute-done.4), channel_id=1, source_target_pairs={{0,1},{1,2},{2,3},{3,4},{4,5},{5,6},{6,7},{7,8},{8,9},{9,10},{10,1... | collective-permute-start | bytes 3145736 | tf_op jit(solution)/shard_map/ppermute | solution.py:46
  170.8 1.0 copy-start.7
  171.8 23.6 %collective-permute-start.6 = (bf16[256,2048]{1,0:T(8,128)(2,1)S(1)}, bf16[256,2048]{1,0:T(8,128)(2,1)S(1)}, u32[]{:S(2)}, u32[]{:S(2)}) collective-permute-start(bf16[256,2048]{1,0:T(8,128)(2,1)S(1)} %collective-permute-done.5), channel_id=1, source_target_pairs={{0,1},{1,2},{2,3},{3,4},{4,5},{5,6},{6,7},{7,8},{8,9},{9,10},{10,1... | collective-permute-start | bytes 3145736 | tf_op jit(solution)/shard_map/ppermute | solution.py:46
  195.5 1.0 copy-start.9
  196.5 22.8 %collective-permute-start.7 = (bf16[256,2048]{1,0:T(8,128)(2,1)S(1)}, bf16[256,2048]{1,0:T(8,128)(2,1)S(1)}, u32[]{:S(2)}, u32[]{:S(2)}) collective-permute-start(bf16[256,2048]{1,0:T(8,128)(2,1)S(1)} %collective-permute-done.6), channel_id=1, source_target_pairs={{0,1},{1,2},{2,3},{3,4},{4,5},{5,6},{6,7},{7,8},{8,9},{9,10},{10,1... | collective-permute-start | bytes 3145736 | tf_op jit(solution)/shard_map/ppermute | solution.py:46
  219.3 1.0 copy-start.11
  220.2 22.3 %collective-permute-start.8 = (bf16[256,2048]{1,0:T(8,128)(2,1)S(1)}, bf16[256,2048]{1,0:T(8,128)(2,1)S(1)}, u32[]{:S(2)}, u32[]{:S(2)}) collective-permute-start(bf16[256,2048]{1,0:T(8,128)(2,1)S(1)} %collective-permute-done.7), channel_id=1, source_target_pairs={{0,1},{1,2},{2,3},{3,4},{4,5},{5,6},{6,7},{7,8},{8,9},{9,10},{10,1... | collective-permute-start | bytes 3145736 | tf_op jit(solution)/shard_map/ppermute | solution.py:46
  242.5 1.1 copy-start.13
  243.5 22.4 %collective-permute-start.9 = (bf16[256,2048]{1,0:T(8,128)(2,1)S(1)}, bf16[256,2048]{1,0:T(8,128)(2,1)S(1)}, u32[]{:S(2)}, u32[]{:S(2)}) collective-permute-start(bf16[256,2048]{1,0:T(8,128)(2,1)S(1)} %collective-permute-done.8), channel_id=1, source_target_pairs={{0,1},{1,2},{2,3},{3,4},{4,5},{5,6},{6,7},{7,8},{8,9},{9,10},{10,1... | collective-permute-start | bytes 3145736 | tf_op jit(solution)/shard_map/ppermute | solution.py:46
  265.9 1.0 copy-start.15
  266.9 23.3 %collective-permute-start.10 = (bf16[256,2048]{1,0:T(8,128)(2,1)S(1)}, bf16[256,2048]{1,0:T(8,128)(2,1)S(1)}, u32[]{:S(2)}, u32[]{:S(2)}) collective-permute-start(bf16[256,2048]{1,0:T(8,128)(2,1)S(1)} %collective-permute-done.9), channel_id=1, source_target_pairs={{0,1},{1,2},{2,3},{3,4},{4,5},{5,6},{6,7},{7,8},{8,9},{9,10},{10,1... | collective-permute-start | bytes 3145736 | tf_op jit(solution)/shard_map/ppermute | solution.py:46
  290.2 29.3 %copy-start.17 = (bf16[256,2048]{1,0:T(8,128)(2,1)}, bf16[256,2048]{1,0:T(8,128)(2,1)S(1)}, u32[]{:S(2)}) copy-start(bf16[256,2048]{1,0:T(8,128)(2,1)S(1)} %collective-permute-done.10) | copy-start | bytes 3145732
  290.2 22.4 %collective-permute-start.11 = (bf16[256,2048]{1,0:T(8,128)(2,1)S(1)}, bf16[256,2048]{1,0:T(8,128)(2,1)}, u32[]{:S(2)}, u32[]{:S(2)}) collective-permute-start(bf16[256,2048]{1,0:T(8,128)(2,1)S(1)} %collective-permute-done.10), channel_id=1, source_target_pairs={{0,1},{1,2},{2,3},{3,4},{4,5},{5,6},{6,7},{7,8},{8,9},{9,10},{10,1... | collective-permute-start | bytes 3145736 | tf_op jit(solution)/shard_map/ppermute | solution.py:46
  292.0 19.0 %all-to-all-start = ((s32[32,1,512]{2,1,0:T(1,128)}), s32[32,1,512]{2,1,0:T(1,128)S(1)}, u32[]{:S(2)}, u32[]{:S(2)}) async-start(s32[32,1,512]{2,1,0:T(1,128)} %reshape.131), calls=%async_computation | async-start | bytes 131072 | tf_op jit(solution)/shard_map/all_to_all | solution.py:18
  299.8 13.7 %copy-start.21 = (pred[8]{0:T(512)(128)(4,1)}, pred[8]{0:T(512)(128)(4,1)S(1)}, u32[]{:S(2)}) copy-start(pred[8]{0:T(512)(128)(4,1)S(1)} %iota_compare_fusion) | copy-start | bytes 28
  312.6 66.9 %collective-permute-start.12 = (bf16[256,2048]{1,0:T(8,128)(2,1)}, bf16[256,2048]{1,0:T(8,128)(2,1)}, u32[]{:S(2)}, u32[]{:S(2)}) collective-permute-start(bf16[256,2048]{1,0:T(8,128)(2,1)} %collective-permute-done.11), channel_id=1, source_target_pairs={{0,1},{1,2},{2,3},{3,4},{4,5},{5,6},{6,7},{7,8},{8,9},{9,10},{10,1... | collective-permute-start | bytes 3145736 | tf_op jit(solution)/shard_map/ppermute | solution.py:46
  315.7 94.3 %copy-start.19 = (bf16[2048]{0:T(1024)(128)(2,1)S(1)}, bf16[2048]{0:T(1024)(128)(2,1)}, u32[]{:S(2)}) copy-start(bf16[2048]{0:T(1024)(128)(2,1)} %param.11) | copy-start | bytes 12292
  315.7 94.3 %copy-start.20 = (bf16[2048]{0:T(1024)(128)(2,1)S(1)}, bf16[2048]{0:T(1024)(128)(2,1)}, u32[]{:S(2)}) copy-start(bf16[2048]{0:T(1024)(128)(2,1)} %param.10) | copy-start | bytes 12292
  319.5 158.2 %copy-start = (bf16[256,2048]{1,0:T(8,128)(2,1)S(1)}, bf16[256,2048]{1,0:T(8,128)(2,1)}, u32[]{:S(2)}) copy-start(bf16[256,2048]{1,0:T(8,128)(2,1)} %param.9) | copy-start | bytes 3145732
  379.4 30.6 %collective-permute-start.13 = (bf16[256,2048]{1,0:T(8,128)(2,1)}, bf16[256,2048]{1,0:T(8,128)(2,1)}, u32[]{:S(2)}, u32[]{:S(2)}) collective-permute-start(bf16[256,2048]{1,0:T(8,128)(2,1)} %collective-permute-done.12), channel_id=1, source_target_pairs={{0,1},{1,2},{2,3},{3,4},{4,5},{5,6},{6,7},{7,8},{8,9},{9,10},{10,1... | collective-permute-start | bytes 3145736 | tf_op jit(solution)/shard_map/ppermute | solution.py:46
  394.9 47.0 %all-to-all-start.1 = ((bf16[32,64,128]{2,1,0:T(8,128)(2,1)}), bf16[32,64,128]{2,1,0:T(8,128)(2,1)}, u32[]{:S(2)}, u32[]{:S(2)}) async-start(bf16[32,64,128]{2,1,0:T(8,128)(2,1)} %bitcast.35), calls=%async_computation.1 | async-start | bytes 1048576 | tf_op jit(solution)/shard_map/all_to_all | solution.py:30
  399.7 101.4 %all-gather.2.cloned.1.call-start = ((), (), s32[]{:S(2)}) async-start(), calls=%async_computation.2 | async-start | bytes 1572864 | tf_op jit(solution)/shard_map/all_gather | solution.py:43
  410.0 34.0 %collective-permute-start.14 = (bf16[256,2048]{1,0:T(8,128)(2,1)}, bf16[256,2048]{1,0:T(8,128)(2,1)}, u32[]{:S(2)}, u32[]{:S(2)}) collective-permute-start(bf16[256,2048]{1,0:T(8,128)(2,1)} %collective-permute-done.13), channel_id=1, source_target_pairs={{0,1},{1,2},{2,3},{3,4},{4,5},{5,6},{6,7},{7,8},{8,9},{9,10},{10,1... | collective-permute-start | bytes 3145736 | tf_op jit(solution)/shard_map/ppermute | solution.py:46
  443.9 44.1 %copy-start.18 = (bf16[256,2048]{1,0:T(8,128)(2,1)S(1)}, bf16[256,2048]{1,0:T(8,128)(2,1)}, u32[]{:S(2)}) copy-start(bf16[256,2048]{1,0:T(8,128)(2,1)} %copy-done.17) | copy-start | bytes 3145732
  443.9 45.2 %copy-start.16 = (bf16[256,2048]{1,0:T(8,128)(2,1)S(1)}, bf16[256,2048]{1,0:T(8,128)(2,1)}, u32[]{:S(2)}) copy-start(bf16[256,2048]{1,0:T(8,128)(2,1)} %copy-done.15) | copy-start | bytes 3145732
  443.9 46.2 %copy-start.14 = (bf16[256,2048]{1,0:T(8,128)(2,1)S(1)}, bf16[256,2048]{1,0:T(8,128)(2,1)}, u32[]{:S(2)}) copy-start(bf16[256,2048]{1,0:T(8,128)(2,1)} %copy-done.13) | copy-start | bytes 3145732
  444.0 47.2 %copy-start.12 = (bf16[256,2048]{1,0:T(8,128)(2,1)S(1)}, bf16[256,2048]{1,0:T(8,128)(2,1)}, u32[]{:S(2)}) copy-start(bf16[256,2048]{1,0:T(8,128)(2,1)} %copy-done.11) | copy-start | bytes 3145732
  444.0 48.4 %copy-start.10 = (bf16[256,2048]{1,0:T(8,128)(2,1)S(1)}, bf16[256,2048]{1,0:T(8,128)(2,1)}, u32[]{:S(2)}) copy-start(bf16[256,2048]{1,0:T(8,128)(2,1)} %copy-done.9) | copy-start | bytes 3145732
  444.0 49.5 %copy-start.8 = (bf16[256,2048]{1,0:T(8,128)(2,1)S(1)}, bf16[256,2048]{1,0:T(8,128)(2,1)}, u32[]{:S(2)}) copy-start(bf16[256,2048]{1,0:T(8,128)(2,1)} %copy-done.7) | copy-start | bytes 3145732
  444.0 50.6 %copy-start.6 = (bf16[256,2048]{1,0:T(8,128)(2,1)S(1)}, bf16[256,2048]{1,0:T(8,128)(2,1)}, u32[]{:S(2)}) copy-start(bf16[256,2048]{1,0:T(8,128)(2,1)} %copy-done.5) | copy-start | bytes 3145732
  444.0 51.6 %copy-start.4 = (bf16[256,2048]{1,0:T(8,128)(2,1)S(1)}, bf16[256,2048]{1,0:T(8,128)(2,1)}, u32[]{:S(2)}) copy-start(bf16[256,2048]{1,0:T(8,128)(2,1)} %copy-done.3) | copy-start | bytes 3145732
  444.0 52.7 %copy-start.2 = (bf16[256,2048]{1,0:T(8,128)(2,1)S(1)}, bf16[256,2048]{1,0:T(8,128)(2,1)}, u32[]{:S(2)}) copy-start(bf16[256,2048]{1,0:T(8,128)(2,1)} %copy-done.1) | copy-start | bytes 3145732
Sparse Core Ops, SparseCore 0:
  444.0 4.9 all-gather.1
